TPU v7x, 32 devices: a whole 2x2x4 slice. The times are simulated.
32 devices in a mesh: shard: 32 (over z, y, x, core).
Axes of the slice: x: 2, y: 2, z: 4, core: 2. Of those that a mesh axis runs over, the one named last changes fastest.
Arguments:
- weights_master: float32 [262144], P('shard'), may hold values from -6 to 6
- first_moment: float32 [262144], P('shard'), may hold values from -1.2 to 1.2
- second_moment: float32 [262144], P('shard'), may hold values from 0.005 to 0.5
- grad_one: float32 [262144], P('shard'), may hold values from -140 to 140
- grad_two: float32 [262144], P('shard'), may hold values from -140 to 140
Outputs:
- gathered_one: bfloat16 [262144], replicated
- gathered_two: bfloat16 [262144], replicated
- master_out: float32 [262144], P('shard')
- first_out: float32 [262144], P('shard')
- second_out: float32 [262144], P('shard')
All inputs are finite; a program needn't handle non-finite values.
Results may differ from a plain program's by a relative error of at most 0.001.
Values may be sent and summed in bfloat16 or wider, within the bound.
A program may use at most 64 MiB of HBM per device.

v0:
```python
import math

import jax
import jax.numpy as jnp
from jax import lax
from jax.sharding import PartitionSpec as P

STEP0 = 100


def square_sum(gradient):
    return jnp.sum(gradient * gradient)


def adam_update(weights, moment_one, moment_two, gradient, total_sq, param_count, step_index):
    clip_limit = 0.25 * math.sqrt(param_count)
    factor = jnp.minimum(1.0, clip_limit / (jnp.sqrt(total_sq) + 1e-06))
    clipped = factor * gradient
    moment_one = 0.9 * moment_one + 0.1 * clipped
    moment_two = 0.95 * moment_two + 0.05 * clipped * clipped
    bias_first = 1.0 - 0.9 ** (STEP0 + step_index)
    bias_second = 1.0 - 0.95 ** (STEP0 + step_index)
    direction = moment_one / bias_first / (jnp.sqrt(moment_two / bias_second) + 1e-08)
    weights = weights - 0.02 * (direction + 0.1 * weights)
    return (weights, moment_one, moment_two)


def on_device(weights_master, first_moment, second_moment, grad_one, grad_two):
    param_count = weights_master.shape[0] * lax.axis_size("shard")
    total_one = lax.psum(square_sum(grad_one), "shard")
    weights, moment_one, moment_two = adam_update(
        weights_master, first_moment, second_moment, grad_one, total_one, param_count, 1
    )
    shard_one = weights.astype(jnp.bfloat16)
    gathered_one = lax.all_gather(shard_one, "shard", axis=0, tiled=True)
    total_two = lax.psum(square_sum(grad_two), "shard")
    weights, moment_one, moment_two = adam_update(
        weights, moment_one, moment_two, grad_two, total_two, param_count, 2
    )
    shard_two = weights.astype(jnp.bfloat16)
    gathered_two = lax.all_gather(shard_two, "shard", axis=0, tiled=True)
    return (gathered_one, gathered_two, weights, moment_one, moment_two)


def solution(mesh):
    return jax.shard_map(
        on_device,
        mesh=mesh,
        in_specs=(P("shard"), P("shard"), P("shard"), P("shard"), P("shard")),
        out_specs=(P(), P(), P("shard"), P("shard"), P("shard")),
        check_vma=False,
    )
```

profile of v0, /device:TPU:0, one launch (start us, length us, event | category | flops | bytes accessed | tf_op | source)
XLA Modules:
  0.0 128.8 jit_solution(13645659195956887968)
XLA Ops:
  0.6 0.0 copy-start
  0.6 0.0 copy-start.1
  0.7 1.4 %multiply_reduce_fusion = (f32[]{:T(128)}, f32[]{:T(128)}) fusion(f32[8192]{0:T(1024)} %param.9, f32[8192]{0:T(1024)} %param.8), kind=kLoop, calls=%fused_computation.6 | loop fusion | flops 32766 | bytes 65544 | tf_op jit(solution)/shard_map/reduce_sum | solution.py:12
  2.1 42.2 %all-reduce = (f32[]{:T(128)}, f32[]{:T(128)}) all-reduce(f32[]{:T(128)} %get-tuple-element.13, f32[]{:T(128)} %get-tuple-element.12), channel_id=1, replica_groups=mesh['shard'=32] {'shard'}, use_global_device_ids=true, to_apply=%region_1.0 | all-reduce | flops 2 | bytes 16 | tf_op jit(solution)/shard_map/psum | solution.py:30
  45.8 0.0 copy-done
  45.8 0.0 copy-done.1
  45.8 1.5 %fusion.2 = (bf16[8192]{0:T(1024)(128)(2,1)S(1)}, f32[8192]{0:T(1024)}, f32[8192]{0:T(1024)}, f32[8192]{0:T(1024)}, bf16[8192]{0:T(1024)(128)(2,1)S(1)}) fusion(f32[8192]{0:T(1024)S(1)} %copy-done, f32[]{:T(128)S(6)} %min.7, f32[8192]{0:T(1024)S(1)} %copy-done.1, f32[]{:T(128)S(6)} %min.6, f32[8192]{0:T(1024)} %param.6, f32[8192]{0:T(1024)} %param.7, ...), kind=kLoop, calls=%fused_computation.10 | loop fusion | flops 278528 | bytes 294920 | tf_op jit(solution)/shard_map/convert_element_type | solution.py:40
  47.3 41.9 %all_gather.7 = bf16[262144]{0:T(1024)(128)(2,1)S(1)} all-gather(bf16[8192]{0:T(1024)(128)(2,1)S(1)} %get-tuple-element.7), channel_id=1, replica_groups=mesh['shard'=32] {'shard'}, dimensions={0}, use_global_device_ids=true | all-gather | bytes 540672 | tf_op jit(solution)/shard_map/all_gather | solution.py:41
  89.1 38.0 %all_gather.6 = bf16[262144]{0:T(1024)(128)(2,1)S(1)} all-gather(bf16[8192]{0:T(1024)(128)(2,1)S(1)} %get-tuple-element.11), channel_id=1, replica_groups=mesh['shard'=32] {'shard'}, dimensions={0}, use_global_device_ids=true | all-gather | bytes 540672 | tf_op jit(solution)/shard_map/all_gather | solution.py:35
  127.2 0.8 copy.12
  128.0 0.8 copy.13
Async XLA Ops:
  0.6 45.1 %copy-start = (f32[8192]{0:T(1024)S(1)}, f32[8192]{0:T(1024)}, u32[]{:S(2)}) copy-start(f32[8192]{0:T(1024)} %param.9) | copy-start | bytes 98308
  0.6 45.1 %copy-start.1 = (f32[8192]{0:T(1024)S(1)}, f32[8192]{0:T(1024)}, u32[]{:S(2)}) copy-start(f32[8192]{0:T(1024)} %param.8) | copy-start | bytes 98308
where the time goes:
time: 129 us
  blocking collectives  122 us (95%)
  other arithmetic  2.91 us (2%)
  between operations  2.13 us (2%)
  local copies, waits for them, and re-layouts  1.66 us (1%)
    psum x1, blocking collectives, on_device(): total_one = lax.psum(square_sum(grad_one), 'shard')  42.2 us
    all_gather x1, blocking collectives, on_device(): gathered_two = lax.all_gather(shard_two, 'shard', axis=0, tiled=True)  41.9 us
    all_gather x1, blocking collectives, on_device(): gathered_one = lax.all_gather(shard_one, 'shard', axis=0, tiled=True)  38 us

commit v1 on v0

v1 whole, which is shorter than its diff:
```python
import functools
import math

import jax
import jax.numpy as jnp
from jax import lax
from jax.experimental import pallas as pl
from jax.experimental.pallas import tpu as pltpu
from jax.sharding import PartitionSpec as P

STEP0 = 100
LANES = 128
PLANE = 8
MESH = pl.DeviceIdType.MESH


def adam_update(weights, moment_one, moment_two, gradient, total_sq, param_count, step_index):
    clip_limit = 0.25 * math.sqrt(param_count)
    factor = jnp.minimum(1.0, clip_limit / (jnp.sqrt(total_sq) + 1e-06))
    clipped = factor * gradient
    moment_one = 0.9 * moment_one + 0.1 * clipped
    moment_two = 0.95 * moment_two + 0.05 * clipped * clipped
    scale_first = 1.0 / (1.0 - 0.9 ** (STEP0 + step_index))
    scale_second = 1.0 / (1.0 - 0.95 ** (STEP0 + step_index))
    direction = moment_one * scale_first / (jnp.sqrt(moment_two * scale_second) + 1e-08)
    weights = weights - 0.02 * (direction + 0.1 * weights)
    return (weights, moment_one, moment_two)


def far_peers(z, depth):
    if depth == 4:
        half = z // 2
        return [z + 1 - 2 * (z % 2), 2 - half, 3 - 3 * half]
    return [lax.rem(z + k, depth) for k in range(1, depth)]


def exchange_kernel(
    n,
    w_hbm, m_hbm, v_hbm, g1_hbm, g2_hbm,
    one_ref, two_ref, w_out, m_out, v_out,
    w_in, m_in, v_in, g1_in, g2_in, sums,
    in_sem, sum_send, sum_recv, send_sem, far_recv, first_recv, second_recv, pair_recv,
):
    me = lax.axis_index("shard")
    depth = n // PLANE
    z, q = me // PLANE, me % PLANE
    y, x, c = q // 4, (q // 2) % 2, q % 2

    def at(z_, y_, x_, c_):
        return ((z_ * 2 + y_) * 2 + x_) * 2 + c_

    zs = far_peers(z, depth)
    plane_peers = [z * PLANE + (q + k) % PLANE for k in range(1, PLANE)]
    z_peers = [p * PLANE + q for p in zs]
    pair = at(z, y, x, 1 - c)
    along_y = at(z, 1 - y, x, c)
    along_x = at(z, y, 1 - x, c)

    barrier = pltpu.get_barrier_semaphore()
    for peer in reversed(plane_peers + z_peers):
        pl.semaphore_signal(barrier, inc=1, device_id=(peer,), device_id_type=MESH)

    loads = [
        pltpu.make_async_copy(src, dst, in_sem.at[i])
        for i, (src, dst) in enumerate(
            [(g1_hbm, g1_in), (g2_hbm, g2_in), (w_hbm, w_in), (m_hbm, m_in), (v_hbm, v_in)]
        )
    ]
    for load in loads:
        load.start()
    loads[0].wait()
    loads[1].wait()
    grad_one, grad_two = g1_in[...], g2_in[...]
    sums[z, q, pl.ds(0, 1), :] = jnp.sum(grad_one * grad_one, axis=0, keepdims=True)
    sums[z, q, pl.ds(1, 1), :] = jnp.sum(grad_two * grad_two, axis=0, keepdims=True)
    for load in loads[2:]:
        load.wait()

    pl.semaphore_wait(barrier, len(plane_peers) + len(z_peers))

    def remote(src, dst, send, recv, peer):
        return pltpu.make_async_remote_copy(
            src_ref=src, dst_ref=dst, send_sem=send, recv_sem=recv,
            device_id=(peer,), device_id_type=MESH,
        )

    own = sums.at[z, q]
    for peer in plane_peers:
        remote(own, own, sum_send.at[0], sum_recv.at[0], peer).start()
    others = sums.at[0, pl.ds(0, PLANE - 1)]
    remote(others, others, sum_send.at[0], sum_recv.at[0], pair).wait_recv()
    plane = sums.at[z]
    for peer in reversed(z_peers):
        remote(plane, plane, sum_send.at[1], sum_recv.at[1], peer).start()
    rest = sums.at[pl.ds(0, depth - 1)]
    remote(rest, rest, sum_send.at[1], sum_recv.at[1], pair).wait_recv()

    totals = jnp.sum(jnp.sum(sums[...], axis=(0, 1)), axis=1, keepdims=True)
    param_count = n * w_in.shape[0] * LANES
    weights, moment_one, moment_two = adam_update(
        w_in[...], m_in[...], v_in[...], grad_one, totals[0:1], param_count, 1
    )
    one_ref[me] = weights.astype(jnp.bfloat16)
    weights, moment_one, moment_two = adam_update(
        weights, moment_one, moment_two, grad_two, totals[1:2], param_count, 2
    )
    two_ref[me] = weights.astype(jnp.bfloat16)
    w_out[...] = weights
    m_out[...] = moment_one
    v_out[...] = moment_two

    halves = [one_ref, two_ref]
    near = [along_y, along_x]
    last = [along_x, along_y]

    def block(h, index):
        return halves[h].at[index]

    def to_far(h, index, peer):
        remote(block(h, index), block(h, index), send_sem.at[h], far_recv.at[h, z], peer).start()

    def to_near(h, index, z_):
        remote(block(h, index), block(h, index), send_sem.at[h], first_recv.at[h, z_], near[h]).start()

    def to_last(h, index, slot):
        remote(block(h, index), block(h, index), send_sem.at[h], second_recv.at[h, slot], last[h]).start()

    def to_pair(h, index):
        remote(block(h, index), block(h, index), send_sem.at[h], pair_recv.at[h], pair).start()

    def arrived(h, index, sem):
        remote(block(h, index), block(h, index), send_sem.at[h], sem, pair).wait_recv()

    turned = [(1 - y, x), (y, 1 - x)]
    opposite = [(y, 1 - x), (1 - y, x)]
    both = [(1 - y, 1 - x), (1 - y, 1 - x)]

    for peer in reversed(z_peers):
        for h in range(2):
            to_far(h, me, peer)
    for h in range(2):
        to_near(h, me, z)
        to_last(h, me, 2 * z)
        to_pair(h, me)

    def from_near(z_):
        for h in range(2):
            index = at(z_, *turned[h], c)
            arrived(h, index, first_recv.at[h, z_])
            to_last(h, index, 2 * z_ + 1)
            to_pair(h, index)

    def from_last(z_, s):
        for h in range(2):
            index = at(z_, *(opposite, both)[s][h], c)
            arrived(h, index, second_recv.at[h, 2 * z_ + s])
            to_pair(h, index)

    from_near(z)
    for p in zs:
        for h in range(2):
            index = at(p, y, x, c)
            arrived(h, index, far_recv.at[h, p])
            to_near(h, index, p)
            to_last(h, index, 2 * p)
            to_pair(h, index)
    from_last(z, 0)
    for p in zs:
        from_near(p)
    from_last(z, 1)
    for p in zs:
        from_last(p, 0)
    for p in zs:
        from_last(p, 1)

    remote(others, others, sum_send.at[0], sum_recv.at[0], pair).wait_send()
    remote(rest, rest, sum_send.at[1], sum_recv.at[1], pair).wait_send()
    for h in range(2):
        half = halves[h].at[pl.ds(0, n // 2)]
        remote(half, half, send_sem.at[h], pair_recv.at[h], pair).wait_recv()
    for h in range(2):
        sent = halves[h].at[pl.ds(0, n - 1)]
        remote(sent, sent, send_sem.at[h], pair_recv.at[h], pair).wait_send()


def store_kernel(count, *refs):
    sems = refs[-1]
    copies = [
        pltpu.make_async_copy(refs[i], refs[count + i], sems.at[i]) for i in range(count)
    ]
    for copy in copies:
        copy.start()
    for copy in copies:
        copy.wait()


def on_device(weights_master, first_moment, second_moment, grad_one, grad_two):
    n = lax.axis_size("shard")
    rows = weights_master.shape[0] // LANES
    depth = n // PLANE
    flat = [a.reshape(rows, LANES) for a in (weights_master, first_moment, second_moment, grad_one, grad_two)]
    shapes = [((n, rows, LANES), jnp.bfloat16)] * 2 + [((rows, LANES), jnp.float32)] * 3
    any_spec = pl.BlockSpec(memory_space=pl.ANY)
    vmem_spec = pl.BlockSpec(memory_space=pltpu.VMEM)
    results = pl.pallas_call(
        functools.partial(exchange_kernel, n),
        out_shape=[pltpu.VMEM(s, d) for s, d in shapes],
        in_specs=[any_spec] * 5,
        out_specs=[vmem_spec] * 5,
        scratch_shapes=[pltpu.VMEM((rows, LANES), jnp.float32)] * 5
        + [
            pltpu.VMEM((depth, PLANE, 2, LANES), jnp.float32),
            pltpu.SemaphoreType.DMA((5,)),
            pltpu.SemaphoreType.DMA((2,)),
            pltpu.SemaphoreType.DMA((2,)),
            pltpu.SemaphoreType.DMA((2,)),
            pltpu.SemaphoreType.DMA((2, depth)),
            pltpu.SemaphoreType.DMA((2, depth)),
            pltpu.SemaphoreType.DMA((2, 2 * depth)),
            pltpu.SemaphoreType.DMA((2,)),
        ],
        compiler_params=pltpu.CompilerParams(
            collective_id=0, has_side_effects=True, vmem_limit_bytes=rows * LANES * 4 * 5 + (2 << 20)
        ),
        name="exchange",
    )(*flat)
    stored = pl.pallas_call(
        functools.partial(store_kernel, 5),
        out_shape=[jax.ShapeDtypeStruct(s, d) for s, d in shapes],
        in_specs=[any_spec] * 5,
        out_specs=[any_spec] * 5,
        scratch_shapes=[pltpu.SemaphoreType.DMA((5,))],
        compiler_params=pltpu.CompilerParams(vmem_limit_bytes=1 << 20),
        name="store",
    )(*results)
    return tuple(a.reshape(-1) for a in stored)


def solution(mesh):
    return jax.shard_map(
        on_device,
        mesh=mesh,
        in_specs=(P("shard"), P("shard"), P("shard"), P("shard"), P("shard")),
        out_specs=(P(), P(), P("shard"), P("shard"), P("shard")),
        check_vma=False,
    )
```

time: 129 us -> 29 us (0.22)
  blocking collectives: 122 us -> 0 us
  Pallas kernels: 0 us -> 24.1 us
  other arithmetic: 2.91 us -> 0 us
  local copies, waits for them, and re-layouts: 1.66 us -> 3.78 us
  between operations: 2.13 us -> 0.65 us
    all_gather x2 -> x0, blocking collectives: 79.9 us -> none  [the longest x1 41.9 us: on_device(): gathered_two = lax.all_gather(shard_two, 'shard', axis=0, tiled=True)]
    psum x1 -> x0, blocking collectives: 42.2 us -> none  [on_device(): total_one = lax.psum(square_sum(grad_one), 'shard')]
    pallas_call x0 -> x2, Pallas kernels: none -> 24.1 us  [the longest x1 23.1 us: on_device(): pl.pallas_call(functools.partial(exchange_kernel, n), out_shape=[pltpu.VM...]
    unnamed x6 -> x10, local copies, waits for them, and re-layouts: 1.66 us -> 3.78 us
    convert_element_type x1 -> x0, other arithmetic: 1.47 us -> none  [on_device(): shard_two = weights.astype(jnp.bfloat16)]
    reduce_sum x1 -> x0, other arithmetic: 1.44 us -> none  [square_sum(): return jnp.sum(gradient * gradient)]
where the time goes in v1:
time: 29 us; the launch traced here: 28.6 us
  Pallas kernels  24.1 us (83%)
  local copies, waits for them, and re-layouts  3.78 us (13%)
  between operations  0.65 us (2%)
    pallas_call x1, Pallas kernels, on_device(): pl.pallas_call(functools.partial(exchange_kernel, n), out_shape=[pltpu.VM...  23.1 us
    unnamed x10, local copies, waits for them, and re-layouts  3.78 us
    pallas_call x1, Pallas kernels, on_device(): pl.pallas_call(functools.partial(store_kernel, 5), out_shape=[jax.ShapeDt...  1.03 us

profile of v1, /device:TPU:0, one launch (start us, length us, event | category | flops | bytes accessed | tf_op | source)
XLA Modules:
  0.0 28.6 jit_solution(12838983712261175165)
XLA Ops:
  0.6 0.0 copy-start
  0.6 0.7 %copy-done = f32[8192]{0:T(1024)S(1)} copy-done((f32[8192]{0:T(1024)S(1)}, f32[8192]{0:T(1024)}, u32[]{:S(2)}) %copy-start) | copy-done | bytes 32792
  1.4 0.0 copy-start.1
  1.4 0.8 %copy-done.1 = f32[8192]{0:T(1024)S(1)} copy-done((f32[8192]{0:T(1024)S(1)}, f32[8192]{0:T(1024)}, u32[]{:S(2)}) %copy-start.1) | copy-done | bytes 32792
  2.1 0.0 copy-start.2
  2.2 0.8 %copy-done.2 = f32[8192]{0:T(1024)S(1)} copy-done((f32[8192]{0:T(1024)S(1)}, f32[8192]{0:T(1024)}, u32[]{:S(2)}) %copy-start.2) | copy-done | bytes 32792
  2.9 0.0 copy-start.3
  2.9 0.8 %copy-done.3 = f32[8192]{0:T(1024)S(1)} copy-done((f32[8192]{0:T(1024)S(1)}, f32[8192]{0:T(1024)}, u32[]{:S(2)}) %copy-start.3) | copy-done | bytes 32792
  3.7 0.0 copy-start.4
  3.7 0.8 %copy-done.4 = f32[8192]{0:T(1024)S(1)} copy-done((f32[8192]{0:T(1024)S(1)}, f32[8192]{0:T(1024)}, u32[]{:S(2)}) %copy-start.4) | copy-done | bytes 32792
  4.4 23.1 %exchange.1 = (bf16[32,64,128]{2,1,0:T(8,128)(2,1)S(1)}, bf16[32,64,128]{2,1,0:T(8,128)(2,1)S(1)}, f32[64,128]{1,0:T(8,128)S(1)}, f32[64,128]{1,0:T(8,128)S(1)}, f32[64,128]{1,0:T(8,128)S(1)}) custom-call(f32[64,128]{1,0:T(8,128)S(1)} %bitcast.10, f32[64,128]{1,0:T(8,128)S(1)} %bitcast.11, f32[64,128]{1,0:T(8,128)S(1)} %bitcast.12, f32[64,128]{1,0:T(8,128)S(1)} %bitcast.13, ...), custom_call_target="tpu_custom_call" | custom-call | tf_op jit(solution)/shard_map/exchange/pallas_call | solution.py:205
  27.5 1.0 %store.1 = (bf16[32,64,128]{2,1,0:T(8,128)(2,1)}, bf16[32,64,128]{2,1,0:T(8,128)(2,1)}, f32[64,128]{1,0:T(8,128)}, f32[64,128]{1,0:T(8,128)}, f32[64,128]{1,0:T(8,128)}) custom-call(bf16[32,64,128]{2,1,0:T(8,128)(2,1)S(1)} %get-tuple-element.15.refs_0_, bf16[32,64,128]{2,1,0:T(8,128)(2,1)S(1)} %get-tuple-element.16.refs_1_, ...), custom_call_target="tpu_custom_call" | custom-call | tf_op jit(solution)/shard_map/store/pallas_call | solution.py:227
Async XLA Ops:
  0.6 0.8 %copy-start = (f32[8192]{0:T(1024)S(1)}, f32[8192]{0:T(1024)}, u32[]{:S(2)}) copy-start(f32[8192]{0:T(1024)} %param.5) | copy-start | bytes 98308
  1.4 0.8 %copy-start.1 = (f32[8192]{0:T(1024)S(1)}, f32[8192]{0:T(1024)}, u32[]{:S(2)}) copy-start(f32[8192]{0:T(1024)} %param.6) | copy-start | bytes 98308
  2.1 0.8 %copy-start.2 = (f32[8192]{0:T(1024)S(1)}, f32[8192]{0:T(1024)}, u32[]{:S(2)}) copy-start(f32[8192]{0:T(1024)} %param.7) | copy-start | bytes 98308
  2.9 0.8 %copy-start.3 = (f32[8192]{0:T(1024)S(1)}, f32[8192]{0:T(1024)}, u32[]{:S(2)}) copy-start(f32[8192]{0:T(1024)} %param.8) | copy-start | bytes 98308
  3.7 0.8 %copy-start.4 = (f32[8192]{0:T(1024)S(1)}, f32[8192]{0:T(1024)}, u32[]{:S(2)}) copy-start(f32[8192]{0:T(1024)} %param.9) | copy-start | bytes 98308

commit v2 on v1

--- a/solution.py
+++ b/solution.py
@@ -11,6 +11,7 @@
 STEP0 = 100
 LANES = 128
 PLANE = 8
+VMEM_BYTES = 67043328
 MESH = pl.DeviceIdType.MESH
 
 
@@ -39,7 +40,7 @@
     w_hbm, m_hbm, v_hbm, g1_hbm, g2_hbm,
     one_ref, two_ref, w_out, m_out, v_out,
     w_in, m_in, v_in, g1_in, g2_in, sums,
-    in_sem, sum_send, sum_recv, send_sem, far_recv, first_recv, second_recv, pair_recv,
+    in_sem, sum_sem, send_sem, far_recv, first_recv, second_recv, pair_recv,
 ):
     me = lax.axis_index("shard")
     depth = n // PLANE
@@ -50,14 +51,14 @@
         return ((z_ * 2 + y_) * 2 + x_) * 2 + c_
 
     zs = far_peers(z, depth)
-    plane_peers = [z * PLANE + (q + k) % PLANE for k in range(1, PLANE)]
     z_peers = [p * PLANE + q for p in zs]
     pair = at(z, y, x, 1 - c)
     along_y = at(z, 1 - y, x, c)
     along_x = at(z, y, 1 - x, c)
 
+    everyone = [(me + k) % n for k in range(1, n)]
     barrier = pltpu.get_barrier_semaphore()
-    for peer in reversed(plane_peers + z_peers):
+    for peer in everyone:
         pl.semaphore_signal(barrier, inc=1, device_id=(peer,), device_id_type=MESH)
 
     loads = [
@@ -71,12 +72,12 @@
     loads[0].wait()
     loads[1].wait()
     grad_one, grad_two = g1_in[...], g2_in[...]
-    sums[z, q, pl.ds(0, 1), :] = jnp.sum(grad_one * grad_one, axis=0, keepdims=True)
-    sums[z, q, pl.ds(1, 1), :] = jnp.sum(grad_two * grad_two, axis=0, keepdims=True)
+    sums[me, pl.ds(0, 1), :] = jnp.sum(grad_one * grad_one, axis=0, keepdims=True)
+    sums[me, pl.ds(1, 1), :] = jnp.sum(grad_two * grad_two, axis=0, keepdims=True)
     for load in loads[2:]:
         load.wait()
 
-    pl.semaphore_wait(barrier, len(plane_peers) + len(z_peers))
+    pl.semaphore_wait(barrier, n - 1)
 
     def remote(src, dst, send, recv, peer):
         return pltpu.make_async_remote_copy(
@@ -84,18 +85,14 @@
             device_id=(peer,), device_id_type=MESH,
         )
 
-    own = sums.at[z, q]
-    for peer in plane_peers:
-        remote(own, own, sum_send.at[0], sum_recv.at[0], peer).start()
-    others = sums.at[0, pl.ds(0, PLANE - 1)]
-    remote(others, others, sum_send.at[0], sum_recv.at[0], pair).wait_recv()
-    plane = sums.at[z]
-    for peer in reversed(z_peers):
-        remote(plane, plane, sum_send.at[1], sum_recv.at[1], peer).start()
-    rest = sums.at[pl.ds(0, depth - 1)]
-    remote(rest, rest, sum_send.at[1], sum_recv.at[1], pair).wait_recv()
-
-    totals = jnp.sum(jnp.sum(sums[...], axis=(0, 1)), axis=1, keepdims=True)
+    own = sums.at[me]
+    for peer in everyone:
+        remote(own, own, sum_sem.at[0], sum_sem.at[1], peer).start()
+    others = sums.at[pl.ds(0, n - 1)]
+    all_sums = remote(others, others, sum_sem.at[0], sum_sem.at[1], pair)
+    all_sums.wait_recv()
+
+    totals = jnp.sum(jnp.sum(sums[...], axis=0), axis=1, keepdims=True)
     param_count = n * w_in.shape[0] * LANES
     weights, moment_one, moment_two = adam_update(
         w_in[...], m_in[...], v_in[...], grad_one, totals[0:1], param_count, 1
@@ -110,6 +107,7 @@
     v_out[...] = moment_two
 
     halves = [one_ref, two_ref]
+    diag = at(z, 1 - y, 1 - x, c)
     near = [along_y, along_x]
     last = [along_x, along_y]
 
@@ -124,6 +122,7 @@
 
     def to_last(h, index, slot):
         remote(block(h, index), block(h, index), send_sem.at[h], second_recv.at[h, slot], last[h]).start()
+        remote(block(h, index), block(h, index), send_sem.at[h], second_recv.at[h, slot + 1], diag).start()
 
     def to_pair(h, index):
         remote(block(h, index), block(h, index), send_sem.at[h], pair_recv.at[h], pair).start()
@@ -147,7 +146,6 @@
         for h in range(2):
             index = at(z_, *turned[h], c)
             arrived(h, index, first_recv.at[h, z_])
-            to_last(h, index, 2 * z_ + 1)
             to_pair(h, index)
 
     def from_last(z_, s):
@@ -173,8 +171,7 @@
     for p in zs:
         from_last(p, 1)
 
-    remote(others, others, sum_send.at[0], sum_recv.at[0], pair).wait_send()
-    remote(rest, rest, sum_send.at[1], sum_recv.at[1], pair).wait_send()
+    all_sums.wait_send()
     for h in range(2):
         half = halves[h].at[pl.ds(0, n // 2)]
         remote(half, half, send_sem.at[h], pair_recv.at[h], pair).wait_recv()
@@ -202,6 +199,8 @@
     shapes = [((n, rows, LANES), jnp.bfloat16)] * 2 + [((rows, LANES), jnp.float32)] * 3
     any_spec = pl.BlockSpec(memory_space=pl.ANY)
     vmem_spec = pl.BlockSpec(memory_space=pltpu.VMEM)
+    held = sum(math.prod(s) * jnp.dtype(d).itemsize for s, d in shapes)
+    grant = min(60 * 1024 * 1024, VMEM_BYTES - held - (1 << 20))
     results = pl.pallas_call(
         functools.partial(exchange_kernel, n),
         out_shape=[pltpu.VMEM(s, d) for s, d in shapes],
@@ -209,9 +208,8 @@
         out_specs=[vmem_spec] * 5,
         scratch_shapes=[pltpu.VMEM((rows, LANES), jnp.float32)] * 5
         + [
-            pltpu.VMEM((depth, PLANE, 2, LANES), jnp.float32),
+            pltpu.VMEM((n, 2, LANES), jnp.float32),
             pltpu.SemaphoreType.DMA((5,)),
-            pltpu.SemaphoreType.DMA((2,)),
             pltpu.SemaphoreType.DMA((2,)),
             pltpu.SemaphoreType.DMA((2,)),
             pltpu.SemaphoreType.DMA((2, depth)),
@@ -220,7 +218,7 @@
             pltpu.SemaphoreType.DMA((2,)),
         ],
         compiler_params=pltpu.CompilerParams(
-            collective_id=0, has_side_effects=True, vmem_limit_bytes=rows * LANES * 4 * 5 + (2 << 20)
+            collective_id=0, has_side_effects=True, vmem_limit_bytes=grant
         ),
         name="exchange",
     )(*flat)

time: 29 us -> 22.7 us (0.78)
  local copies, waits for them, and re-layouts: 3.78 us -> 0 us
  Pallas kernels: 24.1 us -> 21.9 us
    unnamed x10 -> x0, local copies, waits for them, and re-layouts: 3.78 us -> none
    pallas_call x1, Pallas kernels: 23.1 us -> 20.8 us  [on_device(): pl.pallas_call(functools.partial(exchange_kernel, n), out_shape=[pltpu.VM...]
where the time goes in v2:
time: 22.7 us; the launch traced here: 22.5 us
  Pallas kernels  21.9 us (96%)
  between operations  0.64 us (3%)
    pallas_call x1, Pallas kernels, on_device(): pl.pallas_call(functools.partial(exchange_kernel, n), out_shape=[pltpu.VM...  20.8 us
    pallas_call x1, Pallas kernels, on_device(): pl.pallas_call(functools.partial(store_kernel, 5), out_shape=[jax.ShapeDt...  1.03 us

profile of v2, /device:TPU:0, one launch (start us, length us, event | category | flops | bytes accessed | tf_op | source)
XLA Modules:
  0.0 22.5 jit_solution(14684473307563321888)
XLA Ops:
  0.6 20.8 %exchange.1 = (bf16[32,64,128]{2,1,0:T(8,128)(2,1)S(1)}, bf16[32,64,128]{2,1,0:T(8,128)(2,1)S(1)}, f32[64,128]{1,0:T(8,128)S(1)}, f32[64,128]{1,0:T(8,128)S(1)}, f32[64,128]{1,0:T(8,128)S(1)}) custom-call(f32[64,128]{1,0:T(8,128)} %bitcast.10, f32[64,128]{1,0:T(8,128)} %bitcast.11, f32[64,128]{1,0:T(8,128)} %bitcast.12, f32[64,128]{1,0:T(8,128)} %bitcast.13, ...), custom_call_target="tpu_custom_call" | custom-call | tf_op jit(solution)/shard_map/exchange/pallas_call | solution.py:204
  21.5 1.0 %store.1 = (bf16[32,64,128]{2,1,0:T(8,128)(2,1)}, bf16[32,64,128]{2,1,0:T(8,128)(2,1)}, f32[64,128]{1,0:T(8,128)}, f32[64,128]{1,0:T(8,128)}, f32[64,128]{1,0:T(8,128)}) custom-call(bf16[32,64,128]{2,1,0:T(8,128)(2,1)S(1)} %get-tuple-element.15.refs_0_, bf16[32,64,128]{2,1,0:T(8,128)(2,1)S(1)} %get-tuple-element.16.refs_1_, ...), custom_call_target="tpu_custom_call" | custom-call | tf_op jit(solution)/shard_map/store/pallas_call | solution.py:225

commit v3 on v2

--- a/solution.py
+++ b/solution.py
@@ -56,7 +56,8 @@
     along_y = at(z, 1 - y, x, c)
     along_x = at(z, y, 1 - x, c)
 
-    everyone = [(me + k) % n for k in range(1, n)]
+    everyone = [p * PLANE + (q + k) % PLANE for p in zs[::-1] for k in reversed(range(PLANE))]
+    everyone += [z * PLANE + (q + k) % PLANE for k in range(1, PLANE)]
     barrier = pltpu.get_barrier_semaphore()
     for peer in everyone:
         pl.semaphore_signal(barrier, inc=1, device_id=(peer,), device_id_type=MESH)
@@ -154,7 +155,6 @@
             arrived(h, index, second_recv.at[h, 2 * z_ + s])
             to_pair(h, index)
 
-    from_near(z)
     for p in zs:
         for h in range(2):
             index = at(p, y, x, c)
@@ -162,6 +162,7 @@
             to_near(h, index, p)
             to_last(h, index, 2 * p)
             to_pair(h, index)
+    from_near(z)
     from_last(z, 0)
     for p in zs:
         from_near(p)

time: 22.7 us -> 22.6 us (level)
  no operation moved by 1% of the time
where the time goes in v3:
time: 22.6 us; the launch traced here: 22.4 us
  Pallas kernels  21.7 us (96%)
  between operations  0.64 us (3%)
    pallas_call x1, Pallas kernels, on_device(): pl.pallas_call(functools.partial(exchange_kernel, n), out_shape=[pltpu.VM...  20.7 us
    pallas_call x1, Pallas kernels, on_device(): pl.pallas_call(functools.partial(store_kernel, 5), out_shape=[jax.ShapeDt...  1.03 us

profile of v3, /device:TPU:0, one launch (start us, length us, event | category | flops | bytes accessed | tf_op | source)
XLA Modules:
  0.0 22.4 jit_solution(1486292954220791857)
XLA Ops:
  0.6 20.7 %exchange.1 = (bf16[32,64,128]{2,1,0:T(8,128)(2,1)S(1)}, bf16[32,64,128]{2,1,0:T(8,128)(2,1)S(1)}, f32[64,128]{1,0:T(8,128)S(1)}, f32[64,128]{1,0:T(8,128)S(1)}, f32[64,128]{1,0:T(8,128)S(1)}) custom-call(f32[64,128]{1,0:T(8,128)} %bitcast.10, f32[64,128]{1,0:T(8,128)} %bitcast.11, f32[64,128]{1,0:T(8,128)} %bitcast.12, f32[64,128]{1,0:T(8,128)} %bitcast.13, ...), custom_call_target="tpu_custom_call" | custom-call | tf_op jit(solution)/shard_map/exchange/pallas_call | solution.py:205
  21.3 1.0 %store.1 = (bf16[32,64,128]{2,1,0:T(8,128)(2,1)}, bf16[32,64,128]{2,1,0:T(8,128)(2,1)}, f32[64,128]{1,0:T(8,128)}, f32[64,128]{1,0:T(8,128)}, f32[64,128]{1,0:T(8,128)}) custom-call(bf16[32,64,128]{2,1,0:T(8,128)(2,1)S(1)} %get-tuple-element.15.refs_0_, bf16[32,64,128]{2,1,0:T(8,128)(2,1)S(1)} %get-tuple-element.16.refs_1_, ...), custom_call_target="tpu_custom_call" | custom-call | tf_op jit(solution)/shard_map/store/pallas_call | solution.py:226
